TPU v7x, 32 devices: a whole 2x2x4 slice. The times are simulated.
32 devices in a mesh: mem: 8 (over y, x, core), sub: 4 (over z).
Axes of the slice: x: 2, y: 2, z: 4, core: 2. Of those that a mesh axis runs over, the one named last changes fastest.
Arguments:
- control: bfloat16 [64, 1024, 128], P('mem', 'sub'), may hold values from -6 to 6
- perturb: bfloat16 [64, 1024, 128], P('mem', 'sub'), may hold values from -6 to 6
- obs_column: int32 [8, 4, 1024], P('mem', 'sub'), may hold values from 0 to 255
- obs_count: int32 [8, 4], P('mem', 'sub'), may hold values from 128 to 1024, as said below
- obs_background: bfloat16 [8, 4, 1024, 128], P('mem', 'sub'), may hold values from -6 to 6
- obs_value: bfloat16 [8, 4, 1024, 128], P('mem', 'sub'), may hold values from -6 to 6
- obs_weight: float32 [8, 4, 1024], P('mem', 'sub'), may hold values from 0.05 to 0.5
- w_in: bfloat16 [128, 2048], replicated, may hold values from -0.5 to 0.5
- b_in: float32 [2048], replicated, may hold values from -3 to 3
- w_out: bfloat16 [2048, 128], replicated, may hold values from -0.125 to 0.125
Outputs:
- increment: float32 [1024, 128], P(('sub', 'mem'))
- grad_columns: float32 [1024, 128], P(('sub', 'mem'))
Inputs may be any that keep to these rules, and one draw needn't show every extreme that they name: `obs_count`: at least one batch has all 1024 slots live in every draw.
All inputs are finite; a program needn't handle non-finite values.
Results may differ from a plain program's by a relative error of at most 0.0025.
Values sent between devices are 32-bit elements; how exact they have to be, the bound alone decides.
No kernel may reach another device: no remote copies, remote signals or barrier semaphores. Data moves between devices by JAX's collectives and lax.ppermute only.
A program may use at most 64 MiB of HBM per device.

v0:
```python
import jax
import jax.numpy as jnp
from jax import lax
from jax.sharding import PartitionSpec as P

SWEEPS = 4
diffusion = 0.4


def padded_2(block, sides, width):
    for axis, dim in sides:
        count = lax.axis_size(axis)
        forward = [(i, i + 1) for i in range(count - 1)]
        forward.append((count - 1, 0))
        backward = [(target, source) for source, target in forward]
        low = lax.ppermute(
            lax.slice_in_dim(block, block.shape[dim] - width, None, axis=dim), axis, forward
        )
        high = lax.ppermute(lax.slice_in_dim(block, 0, width, axis=dim), axis, backward)
        block = jnp.concatenate([low, block, high], axis=dim)
    return block


def gelu_tanh(values):
    return jax.nn.gelu(values, approximate=True)


def sweep(padded):
    middle = padded[:, 1:-1]
    return middle + diffusion * (padded[:, :-2] - 2.0 * middle + padded[:, 2:])


def observe_block(whole_cols, indices, live, background, targets, weights, w_in, b_in, w_out):
    sampled = jnp.take(whole_cols, indices, axis=0)
    inputs = (background.astype(jnp.float32) + sampled).astype(jnp.bfloat16)
    hidden_pre = jnp.dot(inputs, w_in, preferred_element_type=jnp.float32) + b_in
    hidden, pullback = jax.vjp(gelu_tanh, hidden_pre)
    hidden_low = hidden.astype(jnp.bfloat16)
    outputs = jnp.dot(hidden_low, w_out, preferred_element_type=jnp.float32)
    misfit = ((outputs - targets.astype(jnp.float32)) * (weights * live)[:, None]).astype(
        jnp.bfloat16
    )
    back_hidden = lax.dot_general(
        misfit, w_out, (((1,), (1,)), ((), ())), preferred_element_type=jnp.float32
    )
    (back_pre,) = pullback(back_hidden)
    back_pre = back_pre.astype(jnp.bfloat16)
    back_input = lax.dot_general(
        back_pre, w_in, (((1,), (1,)), ((), ())), preferred_element_type=jnp.float32
    )
    back_input = back_input.astype(jnp.bfloat16)
    column_ids = lax.broadcasted_iota(jnp.int32, (indices.shape[0], whole_cols.shape[0]), 1)
    one_hot = (indices[:, None] == column_ids).astype(jnp.bfloat16)
    return lax.dot_general(
        one_hot, back_input, (((0,), (0,)), ((), ())), preferred_element_type=jnp.float32
    )


def per_device(
    control,
    perturb,
    obs_column,
    obs_count,
    obs_background,
    obs_value,
    obs_weight,
    w_in,
    b_in,
    w_out,
):
    field = control.astype(jnp.float32)
    padded = padded_2(field, (("sub", 1),), SWEEPS)
    for sweep_index in range(SWEEPS):
        padded = sweep(padded)
    field = padded
    partial_sum = jnp.sum(field * perturb.astype(jnp.float32), axis=0)
    members = perturb.shape[0] * lax.axis_size("mem")
    scale = (members - 1) ** (-0.5)
    owned = partial_sum.shape[0] // lax.axis_size("mem")
    whole_cols = lax.psum(partial_sum, "mem") * scale
    increment = lax.dynamic_slice_in_dim(whole_cols, lax.axis_index("mem") * owned, owned, 0)
    indices = obs_column.reshape(-1)
    background = obs_background.reshape(indices.shape[0], -1)
    targets = obs_value.reshape(indices.shape[0], -1)
    weights = obs_weight.reshape(-1)
    live_count = obs_count.reshape(())
    slot_ids = lax.broadcasted_iota(jnp.int32, (indices.shape[0],), 0)
    live = (slot_ids < live_count).astype(jnp.float32)
    gradient = observe_block(
        whole_cols, indices, live, background, targets, weights, w_in, b_in, w_out
    )
    grad_columns = lax.psum_scatter(gradient, "mem", scatter_dimension=0, tiled=True)
    return (increment, grad_columns)


def solution(mesh):
    return jax.shard_map(
        per_device,
        mesh=mesh,
        in_specs=(
            P("mem", "sub", None),
            P("mem", "sub", None),
            P("mem", "sub", None),
            P("mem", "sub"),
            P("mem", "sub", None, None),
            P("mem", "sub", None, None),
            P("mem", "sub", None),
            P(),
            P(),
            P(),
        ),
        out_specs=(P(("sub", "mem"), None), P(("sub", "mem"), None)),
        check_vma=False,
    )
```

profile of v0, /device:TPU:0, one launch (start us, length us, event | category | flops | bytes accessed | tf_op | source)
XLA Modules:
  0.0 135.8 jit_solution(15653344673557643430)
XLA Ops:
  7.2 0.0 all-reduce.2.cloned.1.call-start
  7.2 0.8 fusion.48
  8.0 5.1 %collective-permute-start.1 = (f32[8,4,128]{2,1,0:T(4,128)S(1)}, f32[8,4,128]{2,1,0:T(4,128)S(1)}, u32[]{:S(2)}, u32[]{:S(2)}) collective-permute-start(f32[8,4,128]{2,1,0:T(4,128)S(1)} %get-tuple-element.3), channel_id=1, source_target_pairs={{1,0},{2,1},{3,2},{0,3},{5,4},{6,5},{7,6},{4,7},{9,8},{10,9},{11,1... | collective-permute-start | bytes 49160 | tf_op jit(solution)/shard_map/ppermute | solution.py:19
  13.2 0.7 compare_select_fusion
  14.5 0.7 fusion.36
  15.2 1.1 convert_element_type.35
  16.3 2.4 %collective-permute-done = f32[8,4,128]{2,1,0:T(4,128)S(1)} collective-permute-done((f32[8,4,128]{2,1,0:T(4,128)S(1)}, f32[8,4,128]{2,1,0:T(4,128)S(1)}, u32[]{:S(2)}, u32[]{:S(2)}) %collective-permute-start) | collective-permute-done | bytes 16416 | tf_op jit(solution)/shard_map/ppermute | solution.py:16
  18.7 0.1 pad_maximum_fusion
  18.8 0.3 fusion.23
  19.1 0.3 fusion.21
  19.5 0.3 fusion.19
  19.8 1.1 fusion.27
  20.9 0.0 all-reduce.2.cloned.1.call-update
  20.9 0.0 reduce-scatter.2.cloned.1.call-start
  21.0 52.6 %all-reduce.2.cloned.1.call-done = f32[256,128]{1,0:T(8,128)} async-done(((f32[256,128]{1,0:T(8,128)}), f32[256,128]{1,0:T(8,128)}) %all-reduce.2.cloned.1.call-update) | async-done | bytes 131088 | tf_op jit(solution)/shard_map/psum | solution.py:80
  73.6 0.9 broadcast_multiply_fusion
  74.5 2.8 %gather_fusion = f32[1024,128]{1,0:T(8,128)S(1)} fusion(f32[256,128]{1,0:T(8,128)S(1)} %broadcast_multiply_fusion, s32[1024]{0:T(1024)S(1)} %broadcast_clamp_fusion), kind=kCustom, calls=%fused_computation | custom fusion | bytes 1052672 | tf_op jit(solution)/shard_map/jit(_take)/gather | solution.py:34
  77.4 1.3 fusion.31
  78.7 3.2 %copy-done.1 = f32[1024,2048]{1,0:T(8,128)} copy-done((f32[1024,2048]{1,0:T(8,128)}, f32[1024,2048]{1,0:T(8,128)S(1)}, u32[]{:S(2)}) %copy-start.1) | copy-done | bytes 8388632
  81.9 3.2 %fusion.14 = bf16[1024,128]{1,0:T(8,128)(2,1)S(1)} fusion(bf16[2048,128]{1,0:T(8,128)(2,1)S(1)} %copy-done.5, f32[1024,2048]{1,0:T(8,128)S(1)} %fusion.31, f32[2048]{0:T(1024)S(1)} %copy-done.7, bf16[1,1,1024,128]{3,2,1,0:T(8,128)(2,1)S(1)} %copy-done.6, f32[1024]{0:T(1024)S(1)} %fusion.36), kind=kOutput, calls=%fused_computation.16 | convolution fusion | flops 558366720 | bytes 9449472 | tf_op jit(solution)/shard_map/dot_general | solution.py:39
  85.1 9.4 %fusion.15 = bf16[1024,128]{1,0:T(8,128)(2,1)S(1)} fusion(bf16[128,2048]{1,0:T(8,128)(2,1)S(1)} %copy-done, f32[1024,2048]{1,0:T(8,128)} %copy-done.1, f32[2048]{0:T(1024)S(1)} %copy-done.7, bf16[1024,128]{1,0:T(8,128)(2,1)S(1)} %fusion.14, bf16[2048,128]{1,0:T(8,128)(2,1)S(1)} %copy-done.5), kind=kOutput, calls=%fused_computation.17 | convolution fusion | flops 1117913088 | bytes 9969664 | tf_op jit(solution)/shard_map/dot_general | solution.py:48
  94.6 1.3 fusion.28
  95.9 0.6 constant_dynamic-slice_fusion
  96.5 32.5 %reduce-scatter.2.cloned.1.call-done = f32[32,128]{1,0:T(8,128)} async-done(((f32[256,128]{1,0:T(8,128)}), f32[32,128]{1,0:T(8,128)}) %reduce-scatter.2.cloned.1.call-update) | async-done | bytes 16400 | tf_op jit(solution)/shard_map/reduce_scatter | solution.py:92
  (20 shorter events, 0.1 us)
Async XLA Ops:
  7.2 70.2 %copy-start = (bf16[128,2048]{1,0:T(8,128)(2,1)S(1)}, bf16[128,2048]{1,0:T(8,128)(2,1)}, u32[]{:S(2)}) copy-start(bf16[128,2048]{1,0:T(8,128)(2,1)} %param.17) | copy-start | bytes 1572868
  7.2 66.4 %all-reduce.2.cloned.1.call-start = ((), (), s32[]{:S(2)}) async-start(), calls=%async_computation.1 | async-start | bytes 262144 | tf_op jit(solution)/shard_map/psum | solution.py:80
  8.0 11.8 %copy-start.3 = (bf16[8,256,128]{2,1,0:T(8,128)(2,1)S(1)}, bf16[8,256,128]{2,1,0:T(8,128)(2,1)}, u32[]{:S(2)}) copy-start(bf16[8,256,128]{2,1,0:T(8,128)(2,1)} %param.11) | copy-start | bytes 1572868
  8.0 8.3 %collective-permute-start.1 = (f32[8,4,128]{2,1,0:T(4,128)S(1)}, f32[8,4,128]{2,1,0:T(4,128)S(1)}, u32[]{:S(2)}, u32[]{:S(2)}) collective-permute-start(f32[8,4,128]{2,1,0:T(4,128)S(1)} %get-tuple-element.3), channel_id=1, source_target_pairs={{1,0},{2,1},{3,2},{0,3},{5,4},{6,5},{7,6},{4,7},{9,8},{10,9},{11,1... | collective-permute-start | bytes 49160 | tf_op jit(solution)/shard_map/ppermute | solution.py:19
  13.2 5.5 %collective-permute-start = (f32[8,4,128]{2,1,0:T(4,128)S(1)}, f32[8,4,128]{2,1,0:T(4,128)S(1)}, u32[]{:S(2)}, u32[]{:S(2)}) collective-permute-start(f32[8,4,128]{2,1,0:T(4,128)S(1)} %get-tuple-element.2), channel_id=1, source_target_pairs={{0,1},{1,2},{2,3},{3,0},{4,5},{5,6},{6,7},{7,4},{8,9},{9,10},{10,1... | collective-permute-start | bytes 49160 | tf_op jit(solution)/shard_map/ppermute | solution.py:16
  18.8 2.2 %copy-start.4 = (s32[1,1,1024]{2,1,0:T(1,128)S(1)}, s32[1,1,1024]{2,1,0:T(1,128)}, u32[]{:S(2)}) copy-start(s32[1,1,1024]{2,1,0:T(1,128)} %param.12) | copy-start | bytes 12292
  19.1 58.3 %copy-start.2 = (bf16[1,1,1024,128]{3,2,1,0:T(8,128)(2,1)S(1)}, bf16[1,1,1024,128]{3,2,1,0:T(8,128)(2,1)}, u32[]{:S(2)}) copy-start(bf16[1,1,1024,128]{3,2,1,0:T(8,128)(2,1)} %param.14) | copy-start | bytes 786436
  20.9 108.1 %reduce-scatter.2.cloned.1.call-start = ((), (), s32[]{:S(2)}) async-start(), calls=%async_computation.2 | async-start | bytes 147456 | tf_op jit(solution)/shard_map/reduce_scatter | solution.py:92
  74.5 7.4 %copy-start.5 = (bf16[2048,128]{1,0:T(8,128)(2,1)S(1)}, bf16[2048,128]{1,0:T(8,128)(2,1)}, u32[]{:S(2)}) copy-start(bf16[2048,128]{1,0:T(8,128)(2,1)} %param.19) | copy-start | bytes 1572868
  74.5 7.4 %copy-start.6 = (bf16[1,1,1024,128]{3,2,1,0:T(8,128)(2,1)S(1)}, bf16[1,1,1024,128]{3,2,1,0:T(8,128)(2,1)}, u32[]{:S(2)}) copy-start(bf16[1,1,1024,128]{3,2,1,0:T(8,128)(2,1)} %param.15) | copy-start | bytes 786436
  74.5 7.4 %copy-start.7 = (f32[2048]{0:T(1024)S(1)}, f32[2048]{0:T(1024)}, u32[]{:S(2)}) copy-start(f32[2048]{0:T(1024)} %param.18) | copy-start | bytes 24580
  78.7 3.2 %copy-start.1 = (f32[1024,2048]{1,0:T(8,128)}, f32[1024,2048]{1,0:T(8,128)S(1)}, u32[]{:S(2)}) copy-start(f32[1024,2048]{1,0:T(8,128)S(1)} %fusion.31) | copy-start | bytes 25165828
Sparse Core Ops, SparseCore 0:
  21.0 52.5 all-reduce.1
  96.0 32.9 reduce-scatter.1
where the time goes:
time: 136 us
  waiting for transfers between devices  87.5 us (64%)
  matrix products  15.2 us (11%)
  between operations  14.8 us (11%)
  local copies, waits for them, and re-layouts  7.49 us (6%)
  other arithmetic  5.53 us (4%)
  starting transfers between devices  5.21 us (4%)
    psum x1, waiting for transfers between devices, per_device(): whole_cols = lax.psum(partial_sum, 'mem') * scale  52.6 us
    reduce_scatter x1, waiting for transfers between devices, per_device(): lax.psum_scatter(gradient, 'mem', scatter_dimension=0, tiled=True)  32.5 us
    dot_general x1, matrix products, observe_block(): lax.dot_general(back_pre, w_in, (((1,), (1,)), ((), ())), preferred_eleme...  9.44 us
    ppermute x1, starting transfers between devices, padded_2(): lax.ppermute(lax.slice_in_dim(block, 0, width, axis=dim), axis, backward)  5.13 us
    unnamed x16, local copies, waits for them, and re-layouts  3.27 us
    dot_general x1, matrix products, observe_block(): outputs = jnp.dot(hidden_low, w_out, preferred_element_type=jnp.float32)  3.19 us
    gather x1, local copies, waits for them, and re-layouts, observe_block(): sampled = jnp.take(whole_cols, indices, axis=0)  2.81 us
  transfers between devices with their start and end apart: 4, of which 3 were waited for; matrix products, arithmetic and copies ran while one was open for 2% of the time, Pallas kernels for 0%

commit v1 on v0

--- a/solution.py
+++ b/solution.py
@@ -77,7 +77,7 @@
     members = perturb.shape[0] * lax.axis_size("mem")
     scale = (members - 1) ** (-0.5)
     owned = partial_sum.shape[0] // lax.axis_size("mem")
-    whole_cols = lax.psum(partial_sum, "mem") * scale
+    whole_cols = jnp.sum(lax.all_gather(partial_sum, "mem"), axis=0) * scale
     increment = lax.dynamic_slice_in_dim(whole_cols, lax.axis_index("mem") * owned, owned, 0)
     indices = obs_column.reshape(-1)
     background = obs_background.reshape(indices.shape[0], -1)

time: 136 us -> 106 us (0.78)
  waiting for transfers between devices: 87.5 us -> 58.5 us
    psum x1 -> x0, waiting for transfers between devices: 52.6 us -> none  [per_device(): whole_cols = lax.psum(partial_sum, 'mem') * scale]
    all_gather x0 -> x1, waiting for transfers between devices: none -> 21 us  [per_device(): whole_cols = jnp.sum(lax.all_gather(partial_sum, 'mem'), axis=0) * scale]
    ppermute x1, waiting for transfers between devices: 2.37 us -> 4.09 us  [padded_2(): lax.ppermute(lax.slice_in_dim(block, block.shape[dim] - width, None, axis...]
    unnamed x16 -> x18, local copies, waits for them, and re-layouts: 3.27 us -> 3.27 us
  transfers between devices with their start and end apart: 4 -> 4, of which waited for: 3 -> 4; matrix products, arithmetic and copies ran while one was open for 2% -> 2% of each run, Pallas kernels for 0% -> 0%
where the time goes in v1:
time: 106 us
  waiting for transfers between devices  58.5 us (55%)
  matrix products  15.2 us (14%)
  between operations  14.9 us (14%)
  local copies, waits for them, and re-layouts  7.54 us (7%)
  starting transfers between devices  5.2 us (5%)
  other arithmetic  4.55 us (4%)
    reduce_scatter x1, waiting for transfers between devices, per_device(): lax.psum_scatter(gradient, 'mem', scatter_dimension=0, tiled=True)  33.1 us
    all_gather x1, waiting for transfers between devices, per_device(): whole_cols = jnp.sum(lax.all_gather(partial_sum, 'mem'), axis=0) * scale  21 us
    dot_general x1, matrix products, observe_block(): lax.dot_general(back_pre, w_in, (((1,), (1,)), ((), ())), preferred_eleme...  9.44 us
    ppermute x1, starting transfers between devices, padded_2(): lax.ppermute(lax.slice_in_dim(block, 0, width, axis=dim), axis, backward)  5.12 us
    ppermute x1, waiting for transfers between devices, padded_2(): lax.ppermute(lax.slice_in_dim(block, block.shape[dim] - width, None, axis...  4.09 us
    unnamed x18, local copies, waits for them, and re-layouts  3.27 us
    dot_general x1, matrix products, observe_block(): outputs = jnp.dot(hidden_low, w_out, preferred_element_type=jnp.float32)  3.19 us
    gather x1, local copies, waits for them, and re-layouts, observe_block(): sampled = jnp.take(whole_cols, indices, axis=0)  2.81 us
  transfers between devices with their start and end apart: 4, of which 4 were waited for; matrix products, arithmetic and copies ran while one was open for 2% of the time, Pallas kernels for 0%

profile of v1, /device:TPU:0, one launch (start us, length us, event | category | flops | bytes accessed | tf_op | source)
XLA Modules:
  0.0 105.9 jit_solution(10038672683572871830)
XLA Ops:
  7.2 0.0 all-gather.3.cloned.1.call-start
  7.2 0.8 fusion.48
  8.1 5.1 %collective-permute-start.1 = (f32[8,4,128]{2,1,0:T(4,128)S(1)}, f32[8,4,128]{2,1,0:T(4,128)S(1)}, u32[]{:S(2)}, u32[]{:S(2)}) collective-permute-start(f32[8,4,128]{2,1,0:T(4,128)S(1)} %get-tuple-element.3), channel_id=1, source_target_pairs={{1,0},{2,1},{3,2},{0,3},{5,4},{6,5},{7,6},{4,7},{9,8},{10,9},{11,1... | collective-permute-start | bytes 49160 | tf_op jit(solution)/shard_map/ppermute | solution.py:19
  13.2 1.1 %convert_element_type.35 = f32[8,256,128]{2,1,0:T(8,128)S(1)} convert(bf16[8,256,128]{2,1,0:T(8,128)(2,1)} %param.10) | non-fusion elementwise | flops 262144 | bytes 1572864 | tf_op jit(solution)/shard_map/convert_element_type | solution.py:71
  14.3 0.3 collective-permute-done.1
  14.6 4.1 %collective-permute-done = f32[8,4,128]{2,1,0:T(4,128)S(1)} collective-permute-done((f32[8,4,128]{2,1,0:T(4,128)S(1)}, f32[8,4,128]{2,1,0:T(4,128)S(1)}, u32[]{:S(2)}, u32[]{:S(2)}) %collective-permute-start) | collective-permute-done | bytes 16416 | tf_op jit(solution)/shard_map/ppermute | solution.py:16
  18.7 0.1 pad_maximum_fusion
  18.8 0.3 fusion.23
  19.2 0.3 fusion.21
  19.5 0.3 fusion.19
  19.8 1.1 %fusion.27 = f32[256,128]{1,0:T(8,128)} fusion(f32[8,258,128]{2,1,0:T(8,128)S(1)} %fusion.19, bf16[8,256,128]{2,1,0:T(8,128)(2,1)S(1)} %copy-done.3), kind=kLoop, calls=%fused_computation.35 | loop fusion | flops 2064384 | bytes 3801088 | tf_op jit(solution)/shard_map/reduce_sum | solution.py:76
  20.9 0.0 all-gather.3.cloned.1.call-update
  20.9 0.0 reduce-scatter.2.cloned.1.call-start
  21.7 21.0 %all-gather.3.cloned.1.call-done = f32[2048,128]{1,0:T(8,128)} async-done(((f32[256,128]{1,0:T(8,128)}), f32[2048,128]{1,0:T(8,128)}) %all-gather.3.cloned.1.call-update) | async-done | bytes 1048592 | tf_op jit(solution)/shard_map/all_gather | solution.py:80
  42.7 1.3 %reduce_sum.19 = f32[256,128]{1,0:T(8,128)S(1)} reduce(f32[8,256,128]{2,1,0:T(8,128)} %bitcast.23, f32[]{:T(128)} %constant.19.clone.1), dimensions={0}, to_apply=%region_1.0 | reduce | flops 229376 | bytes 1179652 | tf_op jit(solution)/shard_map/reduce_sum | solution.py:80
  44.0 2.8 %gather_fusion = f32[1024,128]{1,0:T(8,128)S(1)} fusion(f32[256,128]{1,0:T(8,128)S(1)} %broadcast_multiply_fusion, s32[1024]{0:T(1024)S(1)} %broadcast_clamp_fusion), kind=kCustom, calls=%fused_computation | custom fusion | bytes 1052672 | tf_op jit(solution)/shard_map/jit(_take)/gather | solution.py:34
  46.9 1.3 %fusion.31 = f32[1024,2048]{1,0:T(8,128)S(1)} fusion(bf16[128,2048]{1,0:T(8,128)(2,1)S(1)} %copy-done, f32[1024,128]{1,0:T(8,128)S(1)} %gather_fusion, bf16[1,1,1024,128]{3,2,1,0:T(8,128)(2,1)S(1)} %copy-done.2, pred[1024]{0:T(1024)(128)(4,1)S(1)} %compare_and_fusion), kind=kOutput, calls=%fused_computation.42 | convolution fusion | flops 537395200 | bytes 9700352 | tf_op jit(solution)/shard_map/dot_general | solution.py:36
  48.2 3.2 %copy-done.1 = f32[1024,2048]{1,0:T(8,128)} copy-done((f32[1024,2048]{1,0:T(8,128)}, f32[1024,2048]{1,0:T(8,128)S(1)}, u32[]{:S(2)}) %copy-start.1) | copy-done | bytes 8388632
  51.4 3.2 %fusion.14 = bf16[1024,128]{1,0:T(8,128)(2,1)S(1)} fusion(bf16[2048,128]{1,0:T(8,128)(2,1)S(1)} %copy-done.6, f32[1024,2048]{1,0:T(8,128)S(1)} %fusion.31, f32[2048]{0:T(1024)S(1)} %copy-done.8, bf16[1,1,1024,128]{3,2,1,0:T(8,128)(2,1)S(1)} %copy-done.7, f32[1024]{0:T(1024)S(1)} %fusion.36), kind=kOutput, calls=%fused_computation.16 | convolution fusion | flops 558366720 | bytes 9449472 | tf_op jit(solution)/shard_map/dot_general | solution.py:39
  54.6 9.4 %fusion.15 = bf16[1024,128]{1,0:T(8,128)(2,1)S(1)} fusion(bf16[128,2048]{1,0:T(8,128)(2,1)S(1)} %copy-done, f32[1024,2048]{1,0:T(8,128)} %copy-done.1, f32[2048]{0:T(1024)S(1)} %copy-done.8, bf16[1024,128]{1,0:T(8,128)(2,1)S(1)} %fusion.14, bf16[2048,128]{1,0:T(8,128)(2,1)S(1)} %copy-done.6), kind=kOutput, calls=%fused_computation.17 | convolution fusion | flops 1117913088 | bytes 9969664 | tf_op jit(solution)/shard_map/dot_general | solution.py:48
  64.0 1.3 %fusion.28 = f32[256,128]{1,0:T(8,128)} fusion(bf16[1024,128]{1,0:T(8,128)(2,1)S(1)} %fusion.15, s32[1024]{0:T(1024)S(1)} %bitcast.25), kind=kOutput, calls=%fused_computation.38 | convolution fusion | flops 67371008 | bytes 397312 | tf_op jit(solution)/shard_map/dot_general | solution.py:54
  65.3 0.0 reduce-scatter.2.cloned.1.call-update
  65.3 0.6 constant_dynamic-slice_fusion
  66.0 33.1 %reduce-scatter.2.cloned.1.call-done = f32[32,128]{1,0:T(8,128)} async-done(((f32[256,128]{1,0:T(8,128)}), f32[32,128]{1,0:T(8,128)}) %reduce-scatter.2.cloned.1.call-update) | async-done | bytes 16400 | tf_op jit(solution)/shard_map/reduce_scatter | solution.py:92
  (23 shorter events, 0.1 us)
Async XLA Ops:
  7.2 39.7 %copy-start = (bf16[128,2048]{1,0:T(8,128)(2,1)S(1)}, bf16[128,2048]{1,0:T(8,128)(2,1)}, u32[]{:S(2)}) copy-start(bf16[128,2048]{1,0:T(8,128)(2,1)} %param.17) | copy-start | bytes 1572868
  7.2 12.6 %copy-start.3 = (bf16[8,256,128]{2,1,0:T(8,128)(2,1)S(1)}, bf16[8,256,128]{2,1,0:T(8,128)(2,1)}, u32[]{:S(2)}) copy-start(bf16[8,256,128]{2,1,0:T(8,128)(2,1)} %param.11) | copy-start | bytes 1572868
  7.2 35.5 %all-gather.3.cloned.1.call-start = ((), (), s32[]{:S(2)}) async-start(), calls=%async_computation.2 | async-start | bytes 1179648 | tf_op jit(solution)/shard_map/all_gather | solution.py:80
  8.1 6.6 %collective-permute-start.1 = (f32[8,4,128]{2,1,0:T(4,128)S(1)}, f32[8,4,128]{2,1,0:T(4,128)S(1)}, u32[]{:S(2)}, u32[]{:S(2)}) collective-permute-start(f32[8,4,128]{2,1,0:T(4,128)S(1)} %get-tuple-element.3), channel_id=1, source_target_pairs={{1,0},{2,1},{3,2},{0,3},{5,4},{6,5},{7,6},{4,7},{9,8},{10,9},{11,1... | collective-permute-start | bytes 49160 | tf_op jit(solution)/shard_map/ppermute | solution.py:19
  13.2 5.5 %collective-permute-start = (f32[8,4,128]{2,1,0:T(4,128)S(1)}, f32[8,4,128]{2,1,0:T(4,128)S(1)}, u32[]{:S(2)}, u32[]{:S(2)}) collective-permute-start(f32[8,4,128]{2,1,0:T(4,128)S(1)} %get-tuple-element.2), channel_id=1, source_target_pairs={{0,1},{1,2},{2,3},{3,0},{4,5},{5,6},{6,7},{7,4},{8,9},{9,10},{10,1... | collective-permute-start | bytes 49160 | tf_op jit(solution)/shard_map/ppermute | solution.py:16
  18.8 2.8 %copy-start.4 = (s32[1,1,1024]{2,1,0:T(1,128)S(1)}, s32[1,1,1024]{2,1,0:T(1,128)}, u32[]{:S(2)}) copy-start(s32[1,1,1024]{2,1,0:T(1,128)} %param.12) | copy-start | bytes 12292
  18.8 2.9 %copy-start.5 = (f32[1,1,1024]{2,1,0:T(1,128)S(1)}, f32[1,1,1024]{2,1,0:T(1,128)}, u32[]{:S(2)}) copy-start(f32[1,1,1024]{2,1,0:T(1,128)} %param.16) | copy-start | bytes 12292
  19.2 27.7 %copy-start.2 = (bf16[1,1,1024,128]{3,2,1,0:T(8,128)(2,1)S(1)}, bf16[1,1,1024,128]{3,2,1,0:T(8,128)(2,1)}, u32[]{:S(2)}) copy-start(bf16[1,1,1024,128]{3,2,1,0:T(8,128)(2,1)} %param.14) | copy-start | bytes 786436
  20.9 78.1 %reduce-scatter.2.cloned.1.call-start = ((), (), s32[]{:S(2)}) async-start(), calls=%async_computation.1 | async-start | bytes 147456 | tf_op jit(solution)/shard_map/reduce_scatter | solution.py:92
  44.0 7.4 %copy-start.6 = (bf16[2048,128]{1,0:T(8,128)(2,1)S(1)}, bf16[2048,128]{1,0:T(8,128)(2,1)}, u32[]{:S(2)}) copy-start(bf16[2048,128]{1,0:T(8,128)(2,1)} %param.19) | copy-start | bytes 1572868
  44.0 7.4 %copy-start.7 = (bf16[1,1,1024,128]{3,2,1,0:T(8,128)(2,1)S(1)}, bf16[1,1,1024,128]{3,2,1,0:T(8,128)(2,1)}, u32[]{:S(2)}) copy-start(bf16[1,1,1024,128]{3,2,1,0:T(8,128)(2,1)} %param.15) | copy-start | bytes 786436
  44.0 7.4 %copy-start.8 = (f32[2048]{0:T(1024)S(1)}, f32[2048]{0:T(1024)}, u32[]{:S(2)}) copy-start(f32[2048]{0:T(1024)} %param.18) | copy-start | bytes 24580
  48.2 3.2 %copy-start.1 = (f32[1024,2048]{1,0:T(8,128)}, f32[1024,2048]{1,0:T(8,128)S(1)}, u32[]{:S(2)}) copy-start(f32[1024,2048]{1,0:T(8,128)S(1)} %fusion.31) | copy-start | bytes 25165828
Sparse Core Ops, SparseCore 0:
  21.1 21.5 all-gather.2
  65.5 33.5 reduce-scatter.1
